TPU v7x, 32 devices: a whole 2x2x4 slice. The times are simulated.
32 devices in a mesh: prow: 4 (over y, core), pcol: 8 (over z, x).
Axes of the slice: x: 2, y: 2, z: 4, core: 2. Of those that a mesh axis runs over, the one named last changes fastest.
Arguments:
- slab: bfloat16 [8192, 3072], P('prow', 'pcol'), may hold values from -6 to 6
- pivots: int32 [512], replicated, may hold values from 0 to 8191, as said below
- l_top: bfloat16 [512, 512], replicated, may hold values from -0.125 to 0.125
- l_panel_t: bfloat16 [512, 8192], P('pcol', 'prow'), may hold values from -0.125 to 0.125
Outputs:
- result: bfloat16 [8192, 3072], P('prow', 'pcol')
Inputs may be any that keep to these rules, and one draw needn't show every extreme that they name: `pivots`: distinct rows; how many fall on each index of prow is uneven and changes with the draw.
All inputs are finite; a program needn't handle non-finite values.
Results may differ from a plain program's by a relative error of at most 0.0029.
Values may be sent and summed in bfloat16 or wider, within the bound.
A program may use at most 64 MiB of HBM per device.

v0:
```python
import jax
import jax.numpy as jnp
from jax import lax
from jax.sharding import PartitionSpec as P


def spread(block, axis, holder):
    block = jnp.where(lax.axis_index(axis) == holder, block, jnp.zeros_like(block))
    return lax.psum(block, axis)


def bookkeeping(pivots, block):
    index = jnp.arange(block, dtype=jnp.int32)
    chosen = jnp.any(pivots[:, None] == index[None, :], axis=0)
    free = jnp.logical_not(chosen)
    free_rank = jnp.cumsum(free.astype(jnp.int32)) - 1
    far = pivots >= block
    far_rank = jnp.cumsum(far.astype(jnp.int32)) - 1
    match = free[None, :] & (free_rank[None, :] == far_rank[:, None])
    source = jnp.sum(jnp.where(match, index[None, :], 0), axis=1)
    return (far, source)


def unit_solve(lower, right):
    return lax.linalg.triangular_solve(
        lower, right.astype(jnp.float32), left_side=True, lower=True, unit_diagonal=True
    )


def per_device(slab, pivots, l_top, l_panel_t):
    local_rows = slab.shape[0]
    block = pivots.shape[0]
    row_index = lax.axis_index("prow")
    first = row_index * local_rows
    far, source = bookkeeping(pivots, block)
    local_pivot = pivots - first
    mine = (local_pivot >= 0) & (local_pivot < local_rows)
    safe_rows = jnp.clip(local_pivot, 0, local_rows - 1)
    picked = jnp.where(mine[:, None], slab[safe_rows], jnp.zeros((), jnp.bfloat16)).astype(
        jnp.float32
    )
    lower = jnp.tril(l_top.astype(jnp.float32), -1) + jnp.eye(block, dtype=jnp.float32)
    top = lax.psum(picked.astype(jnp.bfloat16), "prow")
    u_block = unit_solve(lower, top).astype(jnp.bfloat16)
    home = spread(slab[:block], "prow", 0)
    target = jnp.where(far & mine, local_pivot, local_rows)
    pivoted = slab.at[target].set(home[source], mode="drop")
    panel = lax.all_gather(l_panel_t, "pcol", axis=0, tiled=True)
    product = lax.dot_general(
        panel, u_block, (((0,), (0,)), ((), ())), preferred_element_type=jnp.float32
    )
    updated = (pivoted.astype(jnp.float32) - product).astype(jnp.bfloat16)
    with_top = updated.at[:block].set(u_block)
    return jnp.where(row_index == 0, with_top, updated)


def solution(mesh):
    return jax.shard_map(
        per_device,
        mesh=mesh,
        in_specs=(P("prow", "pcol"), P(), P(), P("pcol", "prow")),
        out_specs=P("prow", "pcol"),
        check_vma=False,
    )
```

profile of v0, /device:TPU:0, one launch (start us, length us, event | category | flops | bytes accessed | tf_op | source)
XLA Modules:
  0.0 89.4 jit_solution(9014182110018748102)
XLA Ops:
  7.4 0.0 all-reduce.3.cloned.1.call-start
  7.4 1.4 %copy.21 = bf16[2048,384]{1,0:T(8,128)(2,1)S(1)} copy(bf16[2048,384]{1,0:T(8,128)(2,1)} %param.6) | data formatting | bytes 3145728
  8.8 0.0 copy-done.4
  8.8 1.9 %gather_fusion = bf16[512,384]{1,0:T(8,128)(2,1)S(1)} fusion(bf16[2048,384]{1,0:T(8,128)(2,1)S(1)} %copy.21, s32[1024]{0:T(1024)S(1)} %pad_clamp_fusion), kind=kCustom, calls=%fused_computation.1 | custom fusion | bytes 788480 | tf_op jit(solution)/shard_map/gather | solution.py:39
  10.8 0.0 copy-start
  10.8 1.0 %slice_select_fusion.1 = (bf16[512,384]{1,0:T(8,128)(2,1)}, bf16[512,384]{1,0:T(8,128)(2,1)}) fusion(bf16[2048,384]{1,0:T(8,128)(2,1)S(1)} %copy.21, pred[]{:T(512)S(6)} %eq.35, bf16[512,384]{1,0:T(8,128)(2,1)S(1)} %gather_fusion, pred[512]{0:T(512)(128)(4,1)S(1)} %get-tuple-element.38), kind=kLoop, calls=%fused_computation.31 | loop fusion | flops 393216 | bytes 1573377 | tf_op jit(solution)/shard_map/jit(_where)/select_n | solution.py:8
  11.8 0.0 all-reduce.3.cloned.1.call-update
  11.8 0.0 all-gather.2.cloned.1.call-start
  11.9 0.5 all-gather.2.cloned.1.call-update
  12.5 0.0 copy-done
  12.5 0.3 convert_add_fusion
  12.7 7.7 %while.2 = (s32[]{:T(128)}, f32[512,512]{1,0:T(8,128)S(1)}, s32[4,2]{0,1:T(2,128)S(1)}, f32[4,128,128]{2,1,0:T(8,128)S(1)}, s32[]{:T(128)}) while((s32[]{:T(128)}, f32[512,512]{1,0:T(8,128)S(1)}, s32[4,2]{0,1:T(2,128)S(1)}, f32[4,128,128]{2,1,0:T(8,128)S(1)}, s32[]{:T(128)}) %tuple.31), condition=%wide.while_cond.1, body=%wide.while_body.1.sunk | while | flops 2 | bytes 131181 | solution.py:25
  12.8 0.1 constant_dynamic-slice_fusion.2
  12.8 0.5 fusion.34
  13.4 1.3 %bitcast_dynamic-update-slice_fusion.2 = f32[4,128,128]{2,1,0:T(8,128)S(1)} fusion(f32[4,128,128]{2,1,0:T(8,128)S(1)} %get-tuple-element.90, s32[]{:T(128)} %get-tuple-element.87, f32[512,512]{1,0:T(8,128)S(1)} %get-tuple-element.93, s32[]{:T(128)} %bitcast.45, s32[]{:T(128)} %bitcast.46), kind=kLoop, calls=%fused_computation.3.clone.1 | loop fusion | bytes 131084 | tf_op jit(solution)/shard_map/triangular_solve
  14.7 0.1 constant_dynamic-slice_fusion.2
  14.8 0.5 fusion.34
  15.3 1.3 %bitcast_dynamic-update-slice_fusion.2 = f32[4,128,128]{2,1,0:T(8,128)S(1)} fusion(f32[4,128,128]{2,1,0:T(8,128)S(1)} %get-tuple-element.90, s32[]{:T(128)} %get-tuple-element.87, f32[512,512]{1,0:T(8,128)S(1)} %get-tuple-element.93, s32[]{:T(128)} %bitcast.45, s32[]{:T(128)} %bitcast.46), kind=kLoop, calls=%fused_computation.3.clone.1 | loop fusion | bytes 131084 | tf_op jit(solution)/shard_map/triangular_solve
  16.6 0.1 constant_dynamic-slice_fusion.2
  16.7 0.5 fusion.34
  17.2 1.3 %bitcast_dynamic-update-slice_fusion.2 = f32[4,128,128]{2,1,0:T(8,128)S(1)} fusion(f32[4,128,128]{2,1,0:T(8,128)S(1)} %get-tuple-element.90, s32[]{:T(128)} %get-tuple-element.87, f32[512,512]{1,0:T(8,128)S(1)} %get-tuple-element.93, s32[]{:T(128)} %bitcast.45, s32[]{:T(128)} %bitcast.46), kind=kLoop, calls=%fused_computation.3.clone.1 | loop fusion | bytes 131084 | tf_op jit(solution)/shard_map/triangular_solve
  18.5 0.1 constant_dynamic-slice_fusion.2
  18.6 0.5 fusion.34
  19.1 1.3 %bitcast_dynamic-update-slice_fusion.2 = f32[4,128,128]{2,1,0:T(8,128)S(1)} fusion(f32[4,128,128]{2,1,0:T(8,128)S(1)} %get-tuple-element.90, s32[]{:T(128)} %get-tuple-element.87, f32[512,512]{1,0:T(8,128)S(1)} %get-tuple-element.93, s32[]{:T(128)} %bitcast.45, s32[]{:T(128)} %bitcast.46), kind=kLoop, calls=%fused_computation.3.clone.1 | loop fusion | bytes 131084 | tf_op jit(solution)/shard_map/triangular_solve
  20.4 39.9 %custom-call.3 = f32[4,128,128]{1,2,0:T(8,128)} custom-call(f32[4,128,128]{2,1,0:T(8,128)S(1)} %get-tuple-element.24), custom_call_target="InvertDiagBlocksLowerTriangular" | custom-call | tf_op jit(solution)/shard_map/triangular_solve | solution.py:25
  60.4 0.3 reduce-window.24
  60.7 0.1 slice.61
  60.8 0.2 fusion.1
  61.0 0.3 reduce-window.16
  61.3 0.1 slice.59
  61.4 0.1 slice_reduce_fusion
  61.6 0.1 slice_reduce_fusion.1
  61.7 0.1 add_bitcast_fusion
  61.7 0.4 select_reduce_fusion
  62.2 0.0 all-reduce.3.cloned.1.call-done
  62.2 1.0 %convert_element_type.31 = f32[512,384]{1,0:T(8,128)S(1)} convert(bf16[512,384]{1,0:T(8,128)(2,1)} %get-tuple-element.34) | non-fusion elementwise | flops 196608 | bytes 1179648 | tf_op jit(solution)/shard_map/convert_element_type | solution.py:26
  63.2 6.8 %scatter_custom_fusion = bf16[2048,384]{1,0:T(8,128)(2,1)S(1)} fusion(bf16[2048,384]{1,0:T(8,128)(2,1)S(1)} %copy.21, s32[512]{0:T(512)S(1)} %get-tuple-element.40, bf16[512,384]{1,0:T(8,128)(2,1)} %get-tuple-element.33, s32[1024]{0:T(1024)S(1)} %pad_clamp_fusion.1), kind=kCustom, calls=%fused_computation.29 | custom fusion | bytes 1572864 | tf_op jit(solution)/shard_map/scatter | solution.py:47
  70.0 1.3 %fusion.27 = (bf16[128,384]{1,0:T(8,128)(2,1)S(1)}, f32[128,384]{1,0:T(8,128)S(1)}) fusion(bf16[512,384]{1,0:T(8,128)(2,1)} %get-tuple-element.34, f32[4,128,128]{1,2,0:T(8,128)} %custom-call.3), kind=kOutput, calls=%fused_computation.66 | convolution fusion | flops 75546624 | bytes 458752 | tf_op jit(solution)/shard_map/triangular_solve | solution.py:25
  71.3 0.3 convolution_subtract_fusion.2
  71.6 1.8 %fusion.26 = (bf16[128,384]{1,0:T(8,128)(2,1)}, f32[128,384]{1,0:T(8,128)S(1)}) fusion(f32[128,384]{1,0:T(8,128)S(1)} %convolution_subtract_fusion.2, f32[4,128,128]{1,2,0:T(8,128)} %custom-call.3), kind=kOutput, calls=%fused_computation.65 | convolution fusion | flops 75546624 | bytes 557056 | tf_op jit(solution)/shard_map/triangular_solve | solution.py:25
  73.5 0.4 convolution_subtract_fusion.1
  73.9 0.0 copy-done.3
  73.9 1.0 %fusion.25 = (bf16[128,384]{1,0:T(8,128)(2,1)}, f32[128,384]{1,0:T(8,128)S(1)}) fusion(f32[128,384]{1,0:T(8,128)S(1)} %convolution_subtract_fusion.1, f32[4,128,128]{1,2,0:T(8,128)S(1)} %copy-done.3), kind=kOutput, calls=%fused_computation.64 | convolution fusion | flops 75546624 | bytes 557056 | tf_op jit(solution)/shard_map/triangular_solve | solution.py:25
  74.9 0.6 convolution_subtract_fusion
  75.5 0.4 convolution_convert_fusion
  75.8 0.0 all-gather.2.cloned.1.call-done
  75.9 4.2 %fusion = bf16[2048,384]{1,0:T(8,128)(2,1)} fusion(bf16[2048,384]{1,0:T(8,128)(2,1)S(1)} %scatter_custom_fusion, bf16[512,2048]{1,0:T(8,128)(2,1)} %all-gather.2.cloned.1.call-done, bf16[128,384]{1,0:T(8,128)(2,1)S(1)} %convolution_convert_fusion, bf16[128,384]{1,0:T(8,128)(2,1)} %get-tuple-element.43, bf16[128,384]{1,0:T(8,128)(2,1)} %get-tuple-element.45, ...), kind=kOutput, calls=%fused_computation.6 | convolution fusion | flops 809238528 | bytes 5636096 | tf_op jit(solution)/shard_map/dot_general | solution.py:49
  80.1 1.8 %fusion.7 = bf16[2048,384]{1,0:T(8,128)(2,1)} fusion(bf16[2048,384]{1,0:T(8,128)(2,1)} %fusion, pred[]{:T(512)S(6)} %eq.35, bf16[128,384]{1,0:T(8,128)(2,1)S(1)} %convolution_convert_fusion, bf16[128,384]{1,0:T(8,128)(2,1)S(1)} %copy-done.2, bf16[128,384]{1,0:T(8,128)(2,1)S(1)} %copy-done.1, bf16[128,384]{1,0:T(8,128)(2,1)S(1)} %get-tuple-element.47), kind=kLoop, calls=%fused_computation.24 | loop fusion | flops 1769472 | bytes 1179649 | tf_op jit(solution)/shard_map/jit(_where)/select_n | solution.py:54
  (18 shorter events, 0.1 us)
Async XLA Ops:
  7.4 54.8 %all-reduce.3.cloned.1.call-start = ((), (), s32[]{:S(2)}) async-start(), calls=%async_computation.1 | async-start | bytes 1572864 | tf_op jit(solution)/shard_map/psum | solution.py:9
  7.4 1.4 %copy-start.4 = (s32[512]{0:T(512)S(1)}, s32[512]{0:T(512)}, u32[]{:S(2)}) copy-start(s32[512]{0:T(512)} %param.7) | copy-start | bytes 6148
  10.8 1.7 %copy-start = (bf16[512,512]{1,0:T(8,128)(2,1)S(1)}, bf16[512,512]{1,0:T(8,128)(2,1)}, u32[]{:S(2)}) copy-start(bf16[512,512]{1,0:T(8,128)(2,1)} %param.8) | copy-start | bytes 1572868
  11.8 64.0 %all-gather.2.cloned.1.call-start = ((), (), s32[]{:S(2)}) async-start(), calls=%async_computation | async-start | bytes 2359296 | tf_op jit(solution)/shard_map/all_gather | solution.py:48
  70.0 3.8 %copy-start.3 = (f32[4,128,128]{1,2,0:T(8,128)S(1)}, f32[4,128,128]{1,2,0:T(8,128)}, u32[]{:S(2)}) copy-start(f32[4,128,128]{1,2,0:T(8,128)} %custom-call.3) | copy-start | bytes 786436
  75.9 4.2 %copy-start.1 = (bf16[128,384]{1,0:T(8,128)(2,1)S(1)}, bf16[128,384]{1,0:T(8,128)(2,1)}, u32[]{:S(2)}) copy-start(bf16[128,384]{1,0:T(8,128)(2,1)} %get-tuple-element.45) | copy-start | bytes 294916
  75.9 4.2 %copy-start.2 = (bf16[128,384]{1,0:T(8,128)(2,1)S(1)}, bf16[128,384]{1,0:T(8,128)(2,1)}, u32[]{:S(2)}) copy-start(bf16[128,384]{1,0:T(8,128)(2,1)} %get-tuple-element.43) | copy-start | bytes 294916
Sparse Core Ops, SparseCore 0:
  12.0 37.9 all-reduce.2
Sparse Core Ops, SparseCore 1:
  14.5 51.9 all-gather.1
where the time goes:
time: 89.8 us; the launch traced here: 89.4 us
  other arithmetic  45.5 us (51%)
  local copies, waits for them, and re-layouts  18.1 us (20%)
  between operations  15.1 us (17%)
  matrix products  9.97 us (11%)
    another operation x4, other arithmetic, unit_solve(): lax.linalg.triangular_solve(lower, right.astype(jnp.float32), left_side=T...  40.2 us
    another operation x16, local copies, waits for them, and re-layouts  7.98 us
    scatter x1, local copies, waits for them, and re-layouts, per_device(): pivoted = slab.at[target].set(home[source], mode='drop')  6.77 us
    another operation x7, matrix products, unit_solve(): lax.linalg.triangular_solve(lower, right.astype(jnp.float32), left_side=T...  5.75 us
    dot_general x1, matrix products, per_device(): lax.dot_general(panel, u_block, (((0,), (0,)), ((), ())), preferred_eleme...  4.22 us
    gather x1, local copies, waits for them, and re-layouts, per_device(): slab[safe_rows]  1.94 us
    select_n x1, other arithmetic, per_device(): return jnp.where(row_index == 0, with_top, updated)  1.84 us
  transfers between devices with their start and end apart: 2, of which 0 were waited for; matrix products, arithmetic and copies ran while one was open for 71% of the time, Pallas kernels for 0%

commit v1 on v0

v1 whole, which is shorter than its diff:
```python
import functools

import jax
import jax.numpy as jnp
from jax import lax
from jax.experimental import pallas as pl
from jax.experimental.pallas import tpu as pltpu
from jax.sharding import PartitionSpec as P

MESH = pl.DeviceIdType.MESH
F32 = jnp.float32
BF16 = jnp.bfloat16
LANES = 128


def dot(a, b):
    return jnp.dot(a, b, preferred_element_type=F32)


def dot_high(a, b):
    return jnp.dot(a, b, preferred_element_type=F32, precision=lax.Precision.HIGHEST)


def iota(shape, axis):
    return lax.broadcasted_iota(jnp.int32, shape, axis)


def cuts(width):
    units = width // LANES
    first = (units * 7) // 16
    second = (units * 13) // 16
    edges = (0, first * LANES, second * LANES, width)
    return [(a, b - a) for a, b in zip(edges[:-1], edges[1:])]


def kernel(
    n_prow, n_pcol,
    slab_hbm, pivots_ref, l_top_ref, panel_hbm, out_ref,
    slab_ref, gathered, picked, picked_in, merged, homes, pivoted, inverse_hi, inverse_lo, high, u_ref,
    local_sem, panel_recv, panel_send, core_sem, chip_send, chip_recv, relay_send, relay_recv,
):
    block = l_top_ref.shape[0]
    rows, width = slab_ref.shape
    me_r = lax.axis_index("prow")
    me_c = lax.axis_index("pcol")
    chips = n_prow // 2
    chip, core = me_r // 2, me_r % 2
    peer = me_r + 1 - 2 * core
    length = n_pcol // 2
    z, x = me_c // 2, me_c % 2
    other = 1 - x
    pieces = cuts(gathered.shape[2])
    bulk = range(len(pieces) - 1)
    rest = len(pieces) - 1

    slab_copy = pltpu.make_async_copy(slab_hbm, slab_ref, local_sem.at[0])
    panel_copy = pltpu.make_async_copy(panel_hbm, gathered.at[me_c], local_sem.at[1])
    panel_copy.start()
    slab_copy.start()

    barrier = pltpu.get_barrier_semaphore()

    def greet(r, c):
        pl.semaphore_signal(barrier, inc=1, device_id=(r, c), device_id_type=MESH)

    greet(peer, me_c)
    greet(me_r, z * 2 + other)
    for step in range(1, chips):
        greet(((chip + step) % chips) * 2 + core, me_c)

    @pl.when(z > 0)
    def _():
        greet(me_r, me_c - 2)

    @pl.when(z < length - 1)
    def _():
        greet(me_r, me_c + 2)

    has_below = (z + length - 1) // length
    has_above = (2 * length - 2 - z) // length
    pl.semaphore_wait(barrier, 1 + chips + has_below + has_above)

    panel_copy.wait()

    def send(way, source, piece):
        start, size = pieces[piece]
        target = (me_c + 2, me_c - 2, z * 2 + other)[way]
        part = gathered.at[source, :, pl.ds(start, size)]
        return pltpu.make_async_remote_copy(
            src_ref=part, dst_ref=part,
            send_sem=panel_send.at[way, source, piece],
            recv_sem=panel_recv.at[source, piece],
            device_id=(me_r, target), device_id_type=MESH,
        )

    def along(source, piece, ways=(0, 1)):
        if 0 in ways:
            @pl.when(z < length - 1)
            def _():
                send(0, source, piece).start()
        if 1 in ways:
            @pl.when(z > 0)
            def _():
                send(1, source, piece).start()

    def arrived(source, piece):
        send(2, source, piece).wait_recv()

    def first_sends():
        send(2, me_c, rest).start()
        for piece in bulk:
            along(me_c, piece)
            send(2, me_c, piece).start()

    def relay_bulk(distance, piece):
        below = (z - distance) * 2 + x
        above = (z + distance) * 2 + x

        @pl.when(z >= distance)
        def _():
            arrived(below, piece)

            @pl.when(z < length - 1)
            def _():
                send(0, below, piece).start()
            send(2, below, piece).start()

        @pl.when(z < length - distance)
        def _():
            arrived(above, piece)

            @pl.when(z > 0)
            def _():
                send(1, above, piece).start()
            send(2, above, piece).start()

    def own_rest():
        along(me_c, rest)
        arrived(z * 2 + other, rest)
        along(z * 2 + other, rest)

    def relay_rest(distance):
        for side in (x, other):
            below = (z - distance) * 2 + side
            above = (z + distance) * 2 + side

            @pl.when(z >= distance)
            def _():
                arrived(below, rest)

                @pl.when(z < length - 1)
                def _():
                    send(0, below, rest).start()

            @pl.when(z < length - distance)
            def _():
                arrived(above, rest)

                @pl.when(z > 0)
                def _():
                    send(1, above, rest).start()

    def each_line(act):
        for at in range(length):
            act(at)

    def last_arrivals():
        for at in range(length):
            for piece in bulk:
                arrived(at * 2 + other, piece)

    def drain():
        for at in range(length):
            for side in (0, 1):
                source = at * 2 + side
                for piece in range(len(pieces)):
                    def up():
                        send(0, source, piece).wait_send()

                    def down():
                        send(1, source, piece).wait_send()

                    use = (piece == rest) | (x == side)
                    pl.when(use & (z < length - 1) & (at <= z))(up)
                    pl.when(use & (z > 0) & (at >= z))(down)
                    if piece == rest:
                        pl.when((x == side) & (at == z))(lambda: send(2, source, piece).wait_send())
                    else:
                        pl.when(x == side)(lambda: send(2, source, piece).wait_send())

    state = {}
    ii = iota((block, block), 0)
    jj = iota((block, block), 1)

    def column(row):
        return jnp.sum(jnp.where(ii == jj, row, 0.0), axis=1, keepdims=True)

    def bookkeeping():
        pivot_row = pivots_ref[...].astype(F32)
        pivot_col = column(pivot_row)
        chosen = jnp.max(jnp.where(pivot_col == jj.astype(F32), 1.0, 0.0), axis=0, keepdims=True)
        free = 1.0 - chosen
        far = jnp.where(pivot_row >= block, 1.0, 0.0)
        which = iota((16, block), 0)
        both = jnp.where(which == 0, free, jnp.where(which == 1, far, 0.0))
        ranks = dot(both.astype(BF16), jnp.where(ii < jj, 1.0, 0.0).astype(BF16))
        far_rank = column(ranks[1:2])
        match = (free > 0.5) & (ranks[0:1] == far_rank)
        source = jnp.sum(jnp.where(match, jj.astype(F32), 0.0), axis=1, keepdims=True)
        state.update(pivot_row=pivot_row, pivot_col=pivot_col, source=source)

    def pick():
        pivot_col, source = state["pivot_col"], state["source"]
        first = (me_r * rows).astype(F32)
        mine = (pivot_col >= first) & (pivot_col < first + rows)
        lead = (me_r == 0).astype(F32)
        index = jnp.where(mine, pivot_col - first, source * lead - (1.0 - lead))
        slab_copy.wait()
        total = jnp.zeros((block, width), F32)
        for start in range(0, rows, block):
            hot = jnp.where((jj + start).astype(F32) == index, 1.0, 0.0).astype(BF16)
            total = total + dot(hot, slab_ref[start:start + block, :])
        picked[...] = total.astype(BF16)

    def core_copy():
        return pltpu.make_async_remote_copy(
            src_ref=picked, dst_ref=picked_in, send_sem=core_sem.at[0], recv_sem=core_sem.at[1],
            device_id=(peer, me_c), device_id_type=MESH,
        )

    def own_homes():
        homes[:, width:] = jnp.ones((block, LANES), BF16)

        @pl.when(me_r == 0)
        def _():
            hot = jnp.where(jj.astype(F32) == state["source"], 1.0, 0.0).astype(BF16)
            homes[:, :width] = dot(hot, slab_ref[:block, :]).astype(BF16)

    half = block // 2

    def chip_copy(step):
        rows_of = pl.ds(pl.multiple_of(core * half, half), half)
        to = ((chip + step) % chips) * 2 + core
        return pltpu.make_async_remote_copy(
            src_ref=merged.at[0, rows_of], dst_ref=merged.at[step, rows_of],
            send_sem=chip_send.at[step], recv_sem=chip_recv.at[step],
            device_id=(to, me_c), device_id_type=MESH,
        )

    def relay_copy(step):
        part = merged.at[step, pl.ds(pl.multiple_of(core * half, half), half)]
        return pltpu.make_async_remote_copy(
            src_ref=part, dst_ref=part, send_sem=relay_send.at[step], recv_sem=relay_recv.at[step],
            device_id=(peer, me_c), device_id_type=MESH,
        )

    def merge():
        core_copy().wait()
        pivot_col = state["pivot_col"]
        lead = (chip == 0).astype(F32)
        second = jnp.where((pivot_col >= rows) & (pivot_col < 2 * rows), lead, 0.0)
        mine, theirs = picked[...].astype(F32), picked_in[...].astype(F32)
        even = (core == 0).astype(F32)
        keep_mine = 1.0 - even * second
        keep_theirs = 1.0 - (1.0 - even) * second
        merged[0] = (mine * keep_mine + theirs * keep_theirs).astype(BF16)
        for step in range(1, chips):
            chip_copy(step).start()

    def relay_chips():
        for step in range(1, chips):
            chip_copy(step).wait()
            relay_copy(step).start()

    def assemble():
        for step in range(1, chips):
            relay_copy(step).wait()
        pivot_col = state["pivot_col"]
        top = jnp.zeros((block, width), F32)
        for step in range(chips):
            low = (((chip + chips - step) % chips) * 2 * rows).astype(F32)
            here = (pivot_col >= low) & (pivot_col < low + 2 * rows)
            top = top + jnp.where(here, merged[step].astype(F32), 0.0)
        state["top"] = top.astype(BF16)

        @pl.when(me_r == 1)
        def _():
            homes[:, :width] = picked_in[...]

        for step in range(1, chips):
            @pl.when((chip > 0) & (chip == step))
            def _():
                homes[:, :width] = merged[step]

    def interchange(start):
        def act():
            row = iota((block, block), 0) + (me_r * rows + start)
            pivot_row = state["pivot_row"]
            hot = jnp.where((row.astype(F32) == pivot_row) & (pivot_row >= block), 1.0, 0.0)
            both = dot(hot.astype(BF16), homes[...])
            taken = both[:, width:] > 0.5
            for lane in range(0, width, LANES):
                kept = slab_ref[start:start + block, lane:lane + LANES].astype(F32)
                new = jnp.where(taken, both[:, lane:lane + LANES], kept)
                pivoted[start:start + block, lane:lane + LANES] = new.astype(BF16)
        return act

    base = min(block, 256)
    small = min(base, 16)
    bi = iota((base, base), 0)
    bj = iota((base, base), 1)
    groups = block // base

    def diagonal(g):
        part = l_top_ref[g * base:(g + 1) * base, g * base:(g + 1) * base].astype(F32)
        return jnp.where(bi > bj, part, 0.0)

    def start_inverse():
        state["x"], state["power"] = [], []
        for g in range(groups):
            near = jnp.where(bi // small == bj // small, diagonal(g), 0.0)
            state["x"].append(jnp.where(bi == bj, 1.0, 0.0) - near)
            state["power"].append(near)

    def power_step():
        for g in range(groups):
            square = dot_high(state["power"][g], state["power"][g])
            state["power"][g] = square
            state["x"][g] = state["x"][g] + dot_high(state["x"][g], square)

    def double(size):
        def act():
            for g in range(groups):
                link = jnp.where(
                    (bi // (2 * size) == bj // (2 * size)) & (bi // size != bj // size), diagonal(g), 0.0
                )
                inv = state["x"][g]
                state["x"][g] = inv - dot_high(inv, dot_high(link, inv))
        return act

    def join():
        for g in range(groups):
            high[g * base:(g + 1) * base, :] = jnp.zeros((base, block), F32)
            high[g * base:(g + 1) * base, g * base:(g + 1) * base] = state["x"][g]

    def join_double(size):
        def act():
            for at in range(0, block, 2 * size):
                a = high[at:at + size, at:at + size]
                b = high[at + size:at + 2 * size, at + size:at + 2 * size]
                c = l_top_ref[at + size:at + 2 * size, at:at + size].astype(F32)
                high[at + size:at + 2 * size, at:at + size] = -dot_high(b, dot_high(c, a))
        return act

    def split():
        whole = high[...]
        top_bits = whole.astype(BF16)
        inverse_hi[...] = top_bits
        inverse_lo[...] = (whole - top_bits.astype(F32)).astype(BF16)

    def solve():
        top = state["top"]
        u_ref[...] = (dot(inverse_hi[...], top) + dot(inverse_lo[...], top)).astype(BF16)

    inverse = [start_inverse]
    size = 2
    while size < small:
        inverse.append(power_step)
        size *= 2
    size = small
    while size < base:
        inverse.append(double(size))
        size *= 2
    inverse.append(join)
    while size < block:
        inverse.append(join_double(size))
        size *= 2
    inverse.append(split)

    first_sends()
    bookkeeping()
    pick()
    core_copy().start()
    own_homes()
    events = [functools.partial(relay_bulk, d, p) for d in range(1, length) for p in bulk]
    events.append(own_rest)
    events += [functools.partial(relay_rest, d) for d in range(1, length)]
    work = [inverse[0], merge] + inverse[1:7] + [relay_chips] + inverse[7:] + [assemble, solve]
    work += [interchange(start) for start in range(0, rows, block)]
    events.append(last_arrivals)
    per = -(-len(work) // max(1, len(events) - 1))
    for event in events[:-1]:
        event()
        for act in work[:per]:
            act()
        work = work[per:]
    for act in work:
        act()
    events[-1]()

    for start in range(0, rows, block):
        panel = gathered[:, :, start:start + block].reshape(block, block).astype(BF16)
        product = lax.dot_general(
            panel, u_ref[...], (((0,), (0,)), ((), ())), preferred_element_type=F32
        )
        out_ref[start:start + block, :] = (pivoted[start:start + block, :].astype(F32) - product).astype(BF16)

    @pl.when(me_r == 0)
    def _():
        out_ref[:block, :] = u_ref[...]

    drain()


def per_device(n_prow, n_pcol, slab, pivots, l_top, l_panel_t):
    rows, width = slab.shape
    block = pivots.shape[0]
    depth = l_panel_t.shape[0]
    kind = BF16 if depth % 16 == 0 else F32
    panel = l_panel_t.astype(kind)
    chips = n_prow // 2
    n_pieces = len(cuts(rows))
    vmem = pl.BlockSpec(memory_space=pltpu.VMEM)
    anywhere = pl.BlockSpec(memory_space=pl.ANY)
    dma = pltpu.SemaphoreType.DMA
    return pl.pallas_call(
        functools.partial(kernel, n_prow, n_pcol),
        out_shape=jax.ShapeDtypeStruct((rows, width), BF16),
        in_specs=[anywhere, vmem, vmem, anywhere],
        out_specs=vmem,
        scratch_shapes=[
            pltpu.VMEM((rows, width), BF16),
            pltpu.VMEM((n_pcol, depth, rows), kind),
            pltpu.VMEM((block, width), BF16),
            pltpu.VMEM((block, width), BF16),
            pltpu.VMEM((chips, block, width), BF16),
            pltpu.VMEM((block, width + LANES), BF16),
            pltpu.VMEM((rows, width), BF16),
            pltpu.VMEM((block, block), BF16),
            pltpu.VMEM((block, block), BF16),
            pltpu.VMEM((block, block), F32),
            pltpu.VMEM((block, width), BF16),
            dma((2,)),
            dma((n_pcol, n_pieces)),
            dma((3, n_pcol, n_pieces)),
            dma((2,)),
            dma((chips,)),
            dma((chips,)),
            dma((chips,)),
            dma((chips,)),
        ],
        compiler_params=pltpu.CompilerParams(collective_id=0, has_side_effects=True),
    )(slab, pivots.reshape(1, block), l_top, panel)


def solution(mesh):
    return jax.shard_map(
        functools.partial(per_device, mesh.shape["prow"], mesh.shape["pcol"]),
        mesh=mesh,
        in_specs=(P("prow", "pcol"), P(), P(), P("pcol", "prow")),
        out_specs=P("prow", "pcol"),
        check_vma=False,
    )
```

time: 89.8 us -> 40.1 us (0.45)
  other arithmetic: 45.5 us -> 0 us
  Pallas kernels: 0 us -> 37.2 us
  local copies, waits for them, and re-layouts: 18.1 us -> 2.71 us
  between operations: 15.1 us -> 0.01 us
  matrix products: 9.97 us -> 0 us
    another operation x9 -> x0, other arithmetic: 40.9 us -> none  [the longest x4 40.2 us: unit_solve(): lax.linalg.triangular_solve(lower, right.astype(jnp.float32), left_side=T...]
    pallas_call x0 -> x1, Pallas kernels: none -> 37.2 us  [per_device(): pl.pallas_call(functools.partial(kernel, n_prow, n_pcol), out_shape=jax.S...]
    another operation x17 -> x0, local copies, waits for them, and re-layouts: 7.98 us -> none
    scatter x1 -> x0, local copies, waits for them, and re-layouts: 6.77 us -> none  [per_device(): pivoted = slab.at[target].set(home[source], mode='drop')]
    another operation x7 -> x0, matrix products: 5.75 us -> none  [unit_solve(): lax.linalg.triangular_solve(lower, right.astype(jnp.float32), left_side=T...]
    dot_general x1 -> x0, matrix products: 4.22 us -> none  [per_device(): lax.dot_general(panel, u_block, (((0,), (0,)), ((), ())), preferred_eleme...]
    select_n x4 -> x0, other arithmetic: 2.87 us -> none  [the longest x1 1.84 us: per_device(): return jnp.where(row_index == 0, with_top, updated)]
    gather x1 -> x0, local copies, waits for them, and re-layouts: 1.94 us -> none  [per_device(): slab[safe_rows]]
  transfers between devices with their start and end apart: 2 -> 0, of which waited for: 0 -> 0; matrix products, arithmetic and copies ran while one was open for 71% -> 0% of each run, Pallas kernels for 0% -> 0%
where the time goes in v1:
time: 40.1 us; the launch traced here: 39.9 us
  Pallas kernels  37.2 us (93%)
  local copies, waits for them, and re-layouts  2.71 us (7%)
    pallas_call x1, Pallas kernels, per_device(): pl.pallas_call(functools.partial(kernel, n_prow, n_pcol), out_shape=jax.S...  37.2 us
    unnamed x1, local copies, waits for them, and re-layouts  2.71 us

profile of v1, /device:TPU:0, one launch (start us, length us, event | category | flops | bytes accessed | tf_op | source)
XLA Modules:
  0.0 39.9 jit_solution(15593994024916820574)
XLA Ops:
  0.0 37.2 %shard_map.46 = bf16[2048,384]{1,0:T(8,128)(2,1)} custom-call(bf16[2048,384]{1,0:T(8,128)(2,1)} %slab_hbm.1, s32[1,512]{1,0:T(1,128)} %bitcast.1, bf16[512,512]{1,0:T(8,128)(2,1)} %l_top_ref.1, bf16[64,2048]{1,0:T(8,128)(2,1)} %panel_hbm.1), custom_call_target="tpu_custom_call" | custom-call | tf_op jit(solution)/shard_map/pallas_call | solution.py:426
  37.2 2.7 %copy.6 = bf16[2048,384]{1,0:T(8,128)(2,1)} copy(bf16[2048,384]{1,0:T(8,128)(2,1)} %shard_map.46) | data formatting | bytes 3145728

commit v2 on v1

--- a/solution.py
+++ b/solution.py
@@ -13,6 +13,11 @@
 LANES = 128
 
 
+def in_turn(first, second):
+    first()
+    second()
+
+
 def dot(a, b):
     return jnp.dot(a, b, preferred_element_type=F32)
 
@@ -28,15 +33,15 @@
 def cuts(width):
     units = width // LANES
     first = (units * 7) // 16
-    second = (units * 13) // 16
+    second = (units * 14) // 16
     edges = (0, first * LANES, second * LANES, width)
     return [(a, b - a) for a, b in zip(edges[:-1], edges[1:])]
 
 
 def kernel(
     n_prow, n_pcol,
-    slab_hbm, pivots_ref, l_top_ref, panel_hbm, out_ref,
-    slab_ref, gathered, picked, picked_in, merged, homes, pivoted, inverse_hi, inverse_lo, high, u_ref,
+    slab_hbm, pivots_ref, l_top_hbm, panel_hbm, out_ref,
+    slab_ref, l_top_ref, gathered, picked, picked_in, merged, homes, pivoted, inverse_hi, inverse_lo, high, u_ref,
     local_sem, panel_recv, panel_send, core_sem, chip_send, chip_recv, relay_send, relay_recv,
 ):
     block = l_top_ref.shape[0]
@@ -57,6 +62,8 @@
     panel_copy = pltpu.make_async_copy(panel_hbm, gathered.at[me_c], local_sem.at[1])
     panel_copy.start()
     slab_copy.start()
+    l_top_copy = pltpu.make_async_copy(l_top_hbm, l_top_ref, local_sem.at[2])
+    l_top_copy.start()
 
     barrier = pltpu.get_barrier_semaphore()
 
@@ -134,10 +141,17 @@
                 send(1, above, piece).start()
             send(2, above, piece).start()
 
-    def own_rest():
-        along(me_c, rest)
-        arrived(z * 2 + other, rest)
-        along(z * 2 + other, rest)
+    def own_rest(distance):
+        if distance == 0:
+            arrived(z * 2 + other, rest)
+        for source in (me_c, z * 2 + other):
+            @pl.when((z == distance) & (z < length - 1))
+            def _():
+                send(0, source, rest).start()
+
+            @pl.when((length - 1 - z == distance) & (z > 0))
+            def _():
+                send(1, source, rest).start()
 
     def relay_rest(distance):
         for side in (x, other):
@@ -316,6 +330,7 @@
         return jnp.where(bi > bj, part, 0.0)
 
     def start_inverse():
+        l_top_copy.wait()
         state["x"], state["power"] = [], []
         for g in range(groups):
             near = jnp.where(bi // small == bj // small, diagonal(g), 0.0)
@@ -382,9 +397,11 @@
     pick()
     core_copy().start()
     own_homes()
-    events = [functools.partial(relay_bulk, d, p) for d in range(1, length) for p in bulk]
-    events.append(own_rest)
-    events += [functools.partial(relay_rest, d) for d in range(1, length)]
+    events = [functools.partial(own_rest, 0)]
+    for distance in range(1, length):
+        events += [functools.partial(relay_bulk, distance, piece) for piece in bulk]
+        events[-1] = functools.partial(in_turn, events[-1], functools.partial(own_rest, distance))
+    events += [functools.partial(relay_rest, distance) for distance in range(1, length)]
     work = [inverse[0], merge] + inverse[1:7] + [relay_chips] + inverse[7:] + [assemble, solve]
     work += [interchange(start) for start in range(0, rows, block)]
     events.append(last_arrivals)
@@ -421,15 +438,16 @@
     chips = n_prow // 2
     n_pieces = len(cuts(rows))
     vmem = pl.BlockSpec(memory_space=pltpu.VMEM)
-    anywhere = pl.BlockSpec(memory_space=pl.ANY)
+    anywhere = pl.BlockSpec(memory_space=pltpu.HBM)
     dma = pltpu.SemaphoreType.DMA
     return pl.pallas_call(
         functools.partial(kernel, n_prow, n_pcol),
-        out_shape=jax.ShapeDtypeStruct((rows, width), BF16),
-        in_specs=[anywhere, vmem, vmem, anywhere],
+        out_shape=pltpu.VMEM((rows, width), BF16),
+        in_specs=[anywhere, vmem, anywhere, anywhere],
         out_specs=vmem,
         scratch_shapes=[
             pltpu.VMEM((rows, width), BF16),
+            pltpu.VMEM((block, block), BF16),
             pltpu.VMEM((n_pcol, depth, rows), kind),
             pltpu.VMEM((block, width), BF16),
             pltpu.VMEM((block, width), BF16),
@@ -440,7 +458,7 @@
             pltpu.VMEM((block, block), BF16),
             pltpu.VMEM((block, block), F32),
             pltpu.VMEM((block, width), BF16),
-            dma((2,)),
+            dma((3,)),
             dma((n_pcol, n_pieces)),
             dma((3, n_pcol, n_pieces)),
             dma((2,)),
@@ -449,7 +467,7 @@
             dma((chips,)),
             dma((chips,)),
         ],
-        compiler_params=pltpu.CompilerParams(collective_id=0, has_side_effects=True),
+        compiler_params=pltpu.CompilerParams(collective_id=0, has_side_effects=True, vmem_limit_bytes=60 * 2**20),
     )(slab, pivots.reshape(1, block), l_top, panel)
 
 

time: 40.1 us -> 31.9 us (0.80)
  Pallas kernels: 37.2 us -> 30.6 us
  local copies, waits for them, and re-layouts: 2.71 us -> 1.15 us
    pallas_call x1, Pallas kernels: 37.2 us -> 30.6 us  [per_device(): pl.pallas_call(functools.partial(kernel, n_prow, n_pcol), out_shape=pltpu...]
    unnamed x1, local copies, waits for them, and re-layouts: 2.71 us -> 1.15 us
where the time goes in v2:
time: 31.9 us; the launch traced here: 31.8 us
  Pallas kernels  30.6 us (96%)
  local copies, waits for them, and re-layouts  1.15 us (4%)
    pallas_call x1, Pallas kernels, per_device(): pl.pallas_call(functools.partial(kernel, n_prow, n_pcol), out_shape=pltpu...  30.6 us
    unnamed x1, local copies, waits for them, and re-layouts  1.15 us

profile of v2, /device:TPU:0, one launch (start us, length us, event | category | flops | bytes accessed | tf_op | source)
XLA Modules:
  0.0 31.8 jit_solution(1760517387035499591)
XLA Ops:
  0.0 30.6 %shard_map.46 = bf16[2048,384]{1,0:T(8,128)(2,1)S(1)} custom-call(bf16[2048,384]{1,0:T(8,128)(2,1)} %slab_hbm.1, s32[1,512]{1,0:T(1,128)} %bitcast.1, bf16[512,512]{1,0:T(8,128)(2,1)} %l_top_hbm.1, bf16[64,2048]{1,0:T(8,128)(2,1)} %panel_hbm.1), custom_call_target="tpu_custom_call" | custom-call | tf_op jit(solution)/shard_map/pallas_call | solution.py:443
  30.6 1.1 %copy.6 = bf16[2048,384]{1,0:T(8,128)(2,1)} copy(bf16[2048,384]{1,0:T(8,128)(2,1)S(1)} %shard_map.46) | data formatting | bytes 3145728

commit v3 on v2

--- a/solution.py
+++ b/solution.py
@@ -32,9 +32,7 @@
 
 def cuts(width):
     units = width // LANES
-    first = (units * 7) // 16
-    second = (units * 14) // 16
-    edges = (0, first * LANES, second * LANES, width)
+    edges = [(units * part) // 16 * LANES for part in (0, 6, 15, 16)]
     return [(a, b - a) for a, b in zip(edges[:-1], edges[1:])]
 
 

time: 31.9 us -> 31.1 us (0.975)
  Pallas kernels: 30.6 us -> 29.7 us
    pallas_call x1, Pallas kernels: 30.6 us -> 29.7 us  [per_device(): pl.pallas_call(functools.partial(kernel, n_prow, n_pcol), out_shape=pltpu...]
where the time goes in v3:
time: 31.1 us; the launch traced here: 30.9 us
  Pallas kernels  29.7 us (95%)
  local copies, waits for them, and re-layouts  1.15 us (4%)
    pallas_call x1, Pallas kernels, per_device(): pl.pallas_call(functools.partial(kernel, n_prow, n_pcol), out_shape=pltpu...  29.7 us
    unnamed x1, local copies, waits for them, and re-layouts  1.15 us

profile of v3, /device:TPU:0, one launch (start us, length us, event | category | flops | bytes accessed | tf_op | source)
XLA Modules:
  0.0 30.9 jit_solution(13515391228155160597)
XLA Ops:
  0.0 29.7 %shard_map.46 = bf16[2048,384]{1,0:T(8,128)(2,1)S(1)} custom-call(bf16[2048,384]{1,0:T(8,128)(2,1)} %slab_hbm.1, s32[1,512]{1,0:T(1,128)} %bitcast.1, bf16[512,512]{1,0:T(8,128)(2,1)} %l_top_hbm.1, bf16[64,2048]{1,0:T(8,128)(2,1)} %panel_hbm.1), custom_call_target="tpu_custom_call" | custom-call | tf_op jit(solution)/shard_map/pallas_call | solution.py:441
  29.7 1.1 %copy.6 = bf16[2048,384]{1,0:T(8,128)(2,1)} copy(bf16[2048,384]{1,0:T(8,128)(2,1)S(1)} %shard_map.46) | data formatting | bytes 3145728
